TPU v7x, 32 devices: a whole 2x2x4 slice. The times are simulated.
32 devices in a mesh: gx: 2 (over x), gy: 4 (over z), gz: 4 (over y, core).
Axes of the slice: x: 2, y: 2, z: 4, core: 2. Of those that a mesh axis runs over, the one named last changes fastest.
Arguments:
- conductivity: float32 [16, 32, 1024], P('gx', 'gy', 'gz'), may hold values from 0.1 to 10
- source: float32 [16, 32, 1024], P('gx', 'gy', 'gz'), may hold values from -5 to 5
Outputs:
- solution: float32 [16, 32, 1024], P('gx', 'gy', 'gz')
- residual: float32 [16, 32, 1024], P('gx', 'gy', 'gz')
All inputs are finite; a program needn't handle non-finite values.
Results may differ from a plain program's by a relative error of at most 0.0003.
Values sent between devices are 32-bit elements; how exact they have to be, the bound alone decides.
A program may use at most 64 MiB of HBM per device.

v0:
```python
import functools

import jax
import jax.numpy as jnp
from jax import lax
from jax.experimental import pallas as pl
from jax.experimental.pallas import tpu as pltpu
from jax.sharding import PartitionSpec as P

LEVELS = 3
DEGREE = 4
COARSE_DEGREE = 8
MESH = pl.DeviceIdType.MESH


weight_table = {1: 14.0 / 30.0, 2: 3.0 / 30.0, 3: 1.0 / 30.0}
neighbour_offsets = [
    (along_one, along_two, along_three)
    for along_one in (-1, 0, 1)
    for along_two in (-1, 0, 1)
    for along_three in (-1, 0, 1)
    if (along_one, along_two, along_three) != (0, 0, 0)
]
smooth_low = 0.5
coarse_low = 0.03
upper_bound = 2.0


def padded_2(block, sides, width):
    for axis, dim in sides:
        count = lax.axis_size(axis)
        forward = [(i, i + 1) for i in range(count - 1)]
        backward = [(target, source) for source, target in forward]
        low = lax.ppermute(
            lax.slice_in_dim(block, block.shape[dim] - width, None, axis=dim), axis, forward
        )
        high = lax.ppermute(lax.slice_in_dim(block, 0, width, axis=dim), axis, backward)
        block = jnp.concatenate([low, block, high], axis=dim)
    return block


def shifted(padded, offset):
    return padded[
        1 + offset[0] : padded.shape[0] - 1 + offset[0],
        1 + offset[1] : padded.shape[1] - 1 + offset[1],
        1 + offset[2] : padded.shape[2] - 1 + offset[2],
    ]


def inner(values, margin):
    return values[
        margin : values.shape[0] - margin,
        margin : values.shape[1] - margin,
        margin : values.shape[2] - margin,
    ]


def stencil(field_pad, coeff_pad, spacing):
    centre_field = shifted(field_pad, (0, 0, 0))
    centre_coeff = shifted(coeff_pad, (0, 0, 0))
    total = jnp.zeros(centre_field.shape, jnp.float32)
    for offset in neighbour_offsets:
        weight = weight_table[abs(offset[0]) + abs(offset[1]) + abs(offset[2])]
        total = total + weight * (centre_coeff + shifted(coeff_pad, offset)) * (
            centre_field - shifted(field_pad, offset)
        )
    return total * (0.5 / spacing)


def diagonal_of(coeff_pad, spacing):
    centre_coeff = shifted(coeff_pad, (0, 0, 0))
    total = jnp.zeros(centre_coeff.shape, jnp.float32)
    for offset in neighbour_offsets:
        weight = weight_table[abs(offset[0]) + abs(offset[1]) + abs(offset[2])]
        total = total + weight * (centre_coeff + shifted(coeff_pad, offset))
    return total * (0.5 / spacing)


def coarsen(values):
    extent = values.shape
    return values.reshape(extent[0] // 2, 2, extent[1] // 2, 2, extent[2] // 2, 2).mean(
        axis=(1, 3, 5)
    )


def refine(values):
    return jnp.repeat(jnp.repeat(jnp.repeat(values, 2, axis=0), 2, axis=1), 2, axis=2)


def chebyshev_coefs(degree, lower):
    centre = (upper_bound + lower) / 2.0
    half_width = (upper_bound - lower) / 2.0
    ratio_term = centre / half_width
    rho_prev = 1.0 / ratio_term
    weights = []
    for number in range(1, degree):
        rho_next = 1.0 / (2.0 * ratio_term - rho_prev)
        weights.append((rho_next * rho_prev, 2.0 * rho_next / half_width))
        rho_prev = rho_next
    return (centre, weights)


def inside_mask(extent, margin):
    first_pos = (
        lax.axis_index("gx") * extent[0]
        + jnp.arange(extent[0] + 2 * margin, dtype=jnp.int32)
        - margin
    )
    second_pos = (
        lax.axis_index("gy") * extent[1]
        + jnp.arange(extent[1] + 2 * margin, dtype=jnp.int32)
        - margin
    )
    third_pos = (
        lax.axis_index("gz") * extent[2]
        + jnp.arange(extent[2] + 2 * margin, dtype=jnp.int32)
        - margin
    )
    first_ok = (first_pos >= 0) & (first_pos < extent[0] * lax.axis_size("gx"))
    second_ok = (second_pos >= 0) & (second_pos < extent[1] * lax.axis_size("gy"))
    third_ok = (third_pos >= 0) & (third_pos < extent[2] * lax.axis_size("gz"))
    return first_ok[:, None, None] & second_ok[None, :, None] & third_ok[None, None, :]


def operate_near(context, field):
    spacing, coeff_ext, diagonal_ext, inside = context
    padded = padded_2(field, (("gx", 0), ("gy", 1), ("gz", 2)), 1)
    return stencil(padded, inner(coeff_ext, 1), spacing)


def two_steps(context, solution, residual, update, first_pair, second_pair):
    spacing, coeff_ext, diagonal_ext, inside = context
    diagonal = inner(diagonal_ext, 1)
    stacked = jnp.stack([update, residual])
    padded = padded_2(stacked, (("gx", 1), ("gy", 2), ("gz", 3)), 2)
    update_wide = padded[0]
    residual_wide = padded[1]
    residual_near = inner(residual_wide, 1) - stencil(update_wide, coeff_ext, spacing)
    update_near = (
        first_pair[0] * inner(update_wide, 1) + first_pair[1] * residual_near / diagonal_ext
    )
    update_near = jnp.where(inside, update_near, 0.0)
    solution = solution + inner(update_near, 1)
    residual = inner(residual_near, 1) - stencil(update_near, inner(coeff_ext, 1), spacing)
    if second_pair is None:
        update = inner(update_near, 1)
    else:
        update = second_pair[0] * inner(update_near, 1) + second_pair[1] * residual / diagonal
        solution = solution + update
    return (solution, residual, update)


def relax(context, right_side, start, degree, lower, final):
    diagonal = inner(context[2], 1)
    centre, weights = chebyshev_coefs(degree, lower)
    if start is None:
        residual = right_side
    else:
        residual = right_side - operate_near(context, start)
    update = residual / (centre * diagonal)
    solution = update if start is None else start + update
    plan_list = list(weights) + ([None] if final else [])
    position = 0
    while position + 1 < len(plan_list):
        solution, residual, update = two_steps(
            context, solution, residual, update, plan_list[position], plan_list[position + 1]
        )
        position = position + 2
    leftover = plan_list[position:]
    for pair in leftover:
        residual = residual - operate_near(context, update)
        update = pair[0] * update + pair[1] * residual / diagonal
        solution = solution + update
    return (solution, residual)


def body(conductivity, source):
    coeff_now = conductivity
    contexts = []
    for grid_level in range(LEVELS):
        if grid_level > 0:
            coeff_now = coarsen(coeff_now)
        spacing = float(4**grid_level)
        coeff_ext = padded_2(coeff_now, (("gx", 0), ("gy", 1), ("gz", 2)), 2)
        inside = inside_mask(coeff_now.shape, 1)
        diagonal_ext = jnp.where(inside, diagonal_of(coeff_ext, spacing), 1.0)
        contexts.append((spacing, coeff_ext, diagonal_ext, inside))

    def cycle(grid_level, right_side):
        context = contexts[grid_level]
        if grid_level == LEVELS - 1:
            return relax(context, right_side, None, COARSE_DEGREE, coarse_low, False)
        solution, residual = relax(context, right_side, None, DEGREE, smooth_low, True)
        correction, ignored = cycle(grid_level + 1, coarsen(residual))
        solution = solution + refine(correction)
        return relax(context, right_side, solution, DEGREE, smooth_low, grid_level == 0)

    return cycle(0, source)


def cells(shape, dim):
    return lax.broadcasted_iota(jnp.int32, shape, dim)


def pick(left, right):
    if left.dtype == jnp.bfloat16:
        dense, other, swap = right, left, False
    else:
        dense, other, swap = left, right, True
    total = None
    for _ in range(3):
        part = dense.astype(jnp.bfloat16)
        dense = dense - part.astype(jnp.float32)
        pair = (part, other) if swap else (other, part)
        term = jnp.dot(*pair, preferred_element_type=jnp.float32)
        total = term if total is None else total + term
    return total


def ones_where(condition):
    return jnp.where(condition, 1.0, 0.0).astype(jnp.bfloat16)


def turn(values, shift, dim):
    return pltpu.roll(values, shift % values.shape[dim], dim)


def pair_sum(values, dim, edges):
    low = turn(values, 1, dim)
    high = turn(values, -1, dim)
    if edges is not None:
        low = jnp.where(edges[dim][0], 0.0, low)
        high = jnp.where(edges[dim][1], 0.0, high)
    return low + high


def plane_sums(values, edges):
    beside = pair_sum(values, 1, edges)
    strong = 14.0 * values + 3.0 * beside
    weak = 3.0 * values + beside
    return pair_sum(strong, 0, edges) + 14.0 * beside, pair_sum(weak, 0, edges) + strong


class Level:
    def __init__(self, refs, scale, wraps):
        self.k, self.r, self.d, self.di, self.dg, self.e, self.f, self.g = refs
        self.scale = scale
        shape = self.k.shape[1:]
        self.edges = None
        if not wraps:
            self.edges = [
                (cells(shape, dim) == 0, cells(shape, dim) == shape[dim] - 1) for dim in (0, 1)
            ]

    def diagonal(self, wide, near, inside):
        def first(p, carry):
            here, side = plane_sums(self.k[p], self.edges)
            self.e[p] = here
            self.g[p] = side
            return carry

        lax.fori_loop(wide[0], wide[1], first, 0)

        def second(p, carry):
            total = 128.0 * self.k[p] + self.e[p] + self.g[p - 1] + self.g[p + 1]
            total = total * self.scale
            self.dg[p] = total
            good = total > 0.0
            if inside is not None:
                good = good & inside
            self.di[p] = jnp.where(good, 1.0 / total, 0.0)
            return carry

        lax.fori_loop(near[0], near[1], second, 0)

    def first_update(self, span, centre):
        def step(p, carry):
            self.d[p] = self.r[p] * self.di[p] * (1.0 / centre)
            return carry

        lax.fori_loop(span[0], span[1], step, 0)

    def apply(self, wide, near, pair):
        def first(p, carry):
            field = self.d[p]
            coeff = self.k[p]
            here, side = plane_sums(field, self.edges)
            here_k, side_k = plane_sums(coeff * field, self.edges)
            self.e[p] = coeff * here + here_k
            self.f[p] = side
            self.g[p] = side_k
            return carry

        lax.fori_loop(wide[0], wide[1], first, 0)

        def second(p, carry):
            field = self.d[p]
            around = self.e[p] + self.k[p] * (self.f[p - 1] + self.f[p + 1])
            around = around + (self.g[p - 1] + self.g[p + 1])
            left = self.r[p] - (self.dg[p] * field - self.scale * around)
            self.r[p] = left
            if pair is not None:
                fresh = pair[1] * (left * self.di[p])
                self.d[p] = fresh if pair[0] == 0.0 else pair[0] * field + fresh
            return carry

        lax.fori_loop(near[0], near[1], second, 0)


def kernel(sizes, block, *refs):
    (nx, ny, nz) = sizes
    (bx, by, bz) = block
    count = nx * ny * nz
    (k_in, b_in, x_out, r_out) = refs[:4]
    fine_refs = refs[4:12]
    mid_refs = refs[12:20]
    low_refs = refs[20:28]
    (far, x_mid, b_mid, x_low) = refs[28:32]
    (k_send, b_send, r_send, k_got, b_got) = refs[32:37]
    (pack_out, pack_in) = refs[37:39]
    (halo_out, halo_in, z_out, z_in, all_out, all_in) = refs[39:45]
    ix, iy, iz = lax.axis_index("gx"), lax.axis_index("gy"), lax.axis_index("gz")
    me = (ix * ny + iy) * nz + iz
    reach = 5

    def place(number):
        return (number // (ny * nz), (number // nz) % ny, number % nz)

    for ref in (*fine_refs, *mid_refs, *low_refs, far):
        def clear(p, carry, ref=ref):
            ref[p] = jnp.zeros(ref.shape[1:], jnp.float32)
            return carry

        lax.fori_loop(0, ref.shape[0], clear, 0)

    barrier = pltpu.get_barrier_semaphore()

    def greet(j, carry):
        pl.semaphore_signal(
            barrier, inc=1, device_id=place((me + j) % count), device_id_type=MESH
        )
        return carry

    lax.fori_loop(1, count, greet, 0)
    pl.semaphore_wait(barrier, count - 1)

    fine = Level(fine_refs, 0.5 / 30.0, True)
    mid = Level(mid_refs, 0.5 / 4.0 / 30.0, False)
    low = Level(low_refs, 0.5 / 16.0 / 30.0, False)

    def near_copy(source, target, which, dx, dy):
        planes = bx if dx == 0 else reach
        first_from = 0 if dx <= 0 else bx - reach
        first_to = {0: bx, 1: bx - reach, -1: 2 * bx}[dx]
        row_to = {0: 0, 1: 2 * by, -1: by}[dy]
        number = (dx + 1) * 3 + dy + 1
        return pltpu.make_async_remote_copy(
            src_ref=source.at[pl.ds(first_from, planes)],
            dst_ref=target.at[pl.ds(first_to, planes), pl.ds(row_to, by), pl.ds(0, bz)],
            send_sem=halo_out.at[which, number],
            recv_sem=halo_in.at[which, number],
            device_id=(ix + dx, iy + dy, iz),
            device_id_type=MESH,
        )

    sides = [(dx, dy) for dx in (0, 1, -1) for dy in (1, -1, 0) if (dx, dy) != (0, 0)]

    def present(dx, dy):
        return (ix + dx >= 0) & (ix + dx < nx) & (iy + dy >= 0) & (iy + dy < ny)

    def near_start(source, target, which):
        for dx, dy in sides:
            @pl.when(present(dx, dy))
            def _():
                near_copy(source, target, which, dx, dy).start()

    def near_wait(source, target, which):
        for dx, dy in sides:
            @pl.when(present(-dx, -dy))
            def _():
                near_copy(source, target, which, dx, dy).wait_recv()

            @pl.when(present(dx, dy))
            def _():
                near_copy(source, target, which, dx, dy).wait_send()

    lane = cells((3 * by, 128), 1)
    z_planes = list(range(bx - reach, 2 * bx + reach))
    groups = (len(z_planes) + 15) // 16

    def z_copy(which, side):
        return pltpu.make_async_remote_copy(
            src_ref=pack_out.at[which, side],
            dst_ref=pack_in.at[which, side],
            send_sem=z_out.at[which, side],
            recv_sem=z_in.at[which, side],
            device_id=(ix, iy, iz + (1 if side == 0 else -1)),
            device_id_type=MESH,
        )

    to_there = (iz + 1 < nz, iz > 0)
    from_there = (iz > 0, iz + 1 < nz)

    def z_start(window, which):
        for group in range(groups):
            up = jnp.zeros((3 * by, 128), jnp.float32)
            down = jnp.zeros((3 * by, 128), jnp.float32)
            for i, p in enumerate(z_planes[group * 16 : group * 16 + 16]):
                mine = lane // 8 == i
                up = jnp.where(mine, turn(window[p, :, bz - 128 : bz], 8 * i + 8, 1), up)
                down = jnp.where(mine, turn(window[p, :, 0:128], 8 * i, 1), down)
            pack_out[which, 0, group] = up
            pack_out[which, 1, group] = down
        for side in (0, 1):
            @pl.when(to_there[side])
            def _():
                z_copy(which, side).start()

    def z_finish(window, which):
        for side in (0, 1):
            @pl.when(from_there[side])
            def _():
                z_copy(which, side).wait_recv()

            @pl.when(jnp.logical_not(from_there[side]))
            def _():
                pack_in[which, side] = jnp.zeros(pack_in.shape[2:], jnp.float32)

            @pl.when(to_there[side])
            def _():
                z_copy(which, side).wait_send()

        for group in range(groups):
            below = pack_in[which, 0, group]
            above = pack_in[which, 1, group]
            for i, p in enumerate(z_planes[group * 16 : group * 16 + 16]):
                window[p, :, bz : bz + 128] = jnp.where(
                    lane < 64, turn(above, -8 * i, 1), turn(below, -8 * i - 8, 1)
                )

    def all_copy(source, target, which, peer, slot):
        return pltpu.make_async_remote_copy(
            src_ref=source,
            dst_ref=target.at[slot],
            send_sem=all_out.at[which, peer],
            recv_sem=all_in.at[which, slot],
            device_id=place(peer),
            device_id_type=MESH,
        )

    def all_start(source, target, which):
        target[me] = source[...]

        def step(j, carry):
            all_copy(source, target, which, (me + j) % count, me).start()
            return carry

        lax.fori_loop(1, count, step, 0)

    def all_wait(source, target, which):
        def step(j, carry):
            peer = (me + j) % count
            all_copy(source, target, which, peer, peer).wait_recv()
            all_copy(source, target, which, peer, me).wait_send()
            return carry

        lax.fori_loop(1, count, step, 0)

    half = bx // 2 * (by // 2)
    to_row, from_row = cells((half, bx * by), 0), cells((half, bx * by), 1)
    shrink = ones_where(
        (from_row // by // 2 == to_row // (by // 2)) & (from_row % by // 2 == to_row % (by // 2))
    )
    shrink_z = ones_where(cells((bz, bz // 2), 0) // 2 == cells((bz, bz // 2), 1))

    def coarse_block(values):
        flat = pick(pick(shrink, values.reshape(bx * by, bz)), shrink_z) * 0.125
        return flat.reshape(half // 8, 8, bz // 2)

    row8 = cells((8, bz // 2), 0)

    def unpack(got, target):
        for jx in range(nx):
            for jy in range(0, ny, 2):
                for jz in range(nz):
                    slot = (jx * ny + jy) * nz + jz
                    for t in range(half // 8):
                        one, two = got[slot, t], got[slot + nz, t]
                        p = 1 + jx * (bx // 2) + 2 * t
                        at = (slice(jy * 4, jy * 4 + 8), slice(jz * bz // 2, (jz + 1) * bz // 2))
                        target[(p, *at)] = jnp.where(row8 < 4, one, turn(two, 4, 0))
                        target[(p + 1, *at)] = jnp.where(row8 < 4, turn(one, 4, 0), two)

    near_start(k_in, fine.k, 0)
    near_start(b_in, fine.r, 1)
    k_send[...] = coarse_block(k_in[...])
    all_start(k_send, k_got, 0)
    fine.k[bx : 2 * bx, 0:by, 0:bz] = k_in[...]
    fine.r[bx : 2 * bx, 0:by, 0:bz] = b_in[...]
    near_wait(k_in, fine.k, 0)
    z_start(fine.k, 0)
    near_wait(b_in, fine.r, 1)
    z_start(fine.r, 1)
    z_finish(fine.k, 0)

    def span(width):
        return (
            jnp.maximum(bx - width, bx - ix * bx),
            jnp.minimum(2 * bx + width, bx + (nx - ix) * bx),
        )

    plane = (3 * by, bz + 128)
    row, col = cells(plane, 0), cells(plane, 1)
    inside = (
        (row < by) | ((row < 2 * by) & (iy + 1 < ny)) | ((row >= 2 * by) & (iy > 0))
    ) & ((col < bz) | ((col < bz + 64) & (iz + 1 < nz)) | ((col >= bz + 64) & (iz > 0)))
    fine.diagonal(span(5), span(4), inside)
    z_finish(fine.r, 1)

    own = (slice(bx, 2 * bx), slice(0, by), slice(0, bz))
    centre, weights = chebyshev_coefs(DEGREE, smooth_low)
    fine.first_update(span(4), centre)
    x_out[...] = fine.d[own]
    for number in range(DEGREE):
        pair = weights[number] if number < DEGREE - 1 else None
        fine.apply(span(4 - number), span(3 - number), pair)
        if pair is not None:
            x_out[...] += fine.d[own]

    r_send[...] = fine.r[own]
    b_send[...] = coarse_block(r_send[...])
    all_start(b_send, b_got, 1)
    near_start(r_send, far, 2)
    far[own] = r_send[...]

    mx, my, mz = mid.k.shape[0] - 2, mid.k.shape[1], mid.k.shape[2]
    cx, cy, cz = mx // 2, my // 2, mz // 2
    mid_span, low_span = (1, mx + 1), (1, cx + 1)
    all_wait(k_send, k_got, 0)
    unpack(k_got, mid.k)
    mid.diagonal(mid_span, mid_span, None)
    big, small = cells((cx * cy, mx * my), 1), cells((cx * cy, mx * my), 0)
    join = ones_where((big // my // 2 == small // cy) & (big % my // 2 == small % cy))
    join_z = ones_where(cells((mz, cz), 0) // 2 == cells((mz, cz), 1))

    def to_low(values):
        flat = pick(join, pick(values.reshape(mx * my, mz), join_z)) * 0.125
        return flat.reshape(cx, cy, cz)

    low.k[1 : cx + 1] = to_low(mid.k[1 : mx + 1])
    low.diagonal(low_span, low_span, None)

    all_wait(b_send, b_got, 1)
    unpack(b_got, b_mid)
    mid.r[1 : mx + 1] = b_mid[1 : mx + 1]
    mid.first_update(mid_span, centre)
    x_mid[...] = mid.d[1 : mx + 1]
    for number in range(DEGREE):
        pair = weights[number] if number < DEGREE - 1 else None
        mid.apply(mid_span, mid_span, pair)
        if pair is not None:
            x_mid[...] += mid.d[1 : mx + 1]

    near_wait(r_send, far, 2)
    z_start(far, 2)

    low.r[1 : cx + 1] = to_low(mid.r[1 : mx + 1])
    low_centre, low_weights = chebyshev_coefs(COARSE_DEGREE, coarse_low)
    low.first_update(low_span, low_centre)
    x_low[...] = low.d[1 : cx + 1]
    for pair in low_weights:
        low.apply(low_span, low_span, pair)
        x_low[...] += low.d[1 : cx + 1]

    spread = ones_where(
        (cells((mx * my, cx * cy), 0) // my // 2 == cells((mx * my, cx * cy), 1) // cy)
        & (cells((mx * my, cx * cy), 0) % my // 2 == cells((mx * my, cx * cy), 1) % cy)
    )
    spread_z = ones_where(cells((cz, mz), 0) == cells((cz, mz), 1) // 2)
    fixed = pick(spread, pick(x_low[...].reshape(cx * cy, cz), spread_z))
    mid.d[1 : mx + 1] = x_mid[...] + fixed.reshape(mx, my, mz)
    mid.r[1 : mx + 1] = b_mid[1 : mx + 1]
    x_mid[...] = mid.d[1 : mx + 1]
    mid.apply(mid_span, mid_span, (0.0, 1.0 / centre))
    x_mid[...] += mid.d[1 : mx + 1]
    for pair in weights:
        mid.apply(mid_span, mid_span, pair)
        x_mid[...] += mid.d[1 : mx + 1]

    z_finish(far, 2)
    wide = bx + bx // 2
    shape = (wide * 3 * by, mx * my)
    fine_row, mid_row = cells(shape, 0) % (3 * by), cells(shape, 1)
    fine_y = iy * by + jnp.where(fine_row < 2 * by, fine_row, fine_row - 3 * by)
    mid_x = ix * (bx // 2) + cells(shape, 0) // (3 * by) - bx // 2
    rows = ones_where((mid_row // my == mid_x) & (2 * (mid_row % my) == fine_y - fine_y % 2))
    shape = (mz, bz + 128)
    fine_col = cells(shape, 1)
    fine_z = iz * bz + jnp.where(fine_col < bz + 64, fine_col, fine_col - (bz + 128))
    columns = ones_where((fine_z >= 2 * cells(shape, 0)) & (fine_z <= 2 * cells(shape, 0) + 1))
    fixed = pick(rows, pick(x_mid[...].reshape(mx * my, mz), columns))
    fixed = fixed.reshape(wide, 3 * by, bz + 128)
    for p in range(bx - reach, 2 * bx + reach):
        fine.d[p] = fixed[p // 2]
    x_out[...] += fine.d[own]

    def restore(p, carry):
        fine.r[p] = far[p]
        return carry

    lax.fori_loop(*span(4), restore, 0)
    fine.apply(span(5), span(4), (0.0, 1.0 / centre))
    x_out[...] += fine.d[own]
    for number in range(DEGREE):
        pair = weights[number] if number < DEGREE - 1 else None
        fine.apply(span(4 - number), span(3 - number), pair)
        if pair is not None:
            x_out[...] += fine.d[own]
    r_out[...] = fine.r[own]


def gathered(sizes, conductivity, source):
    (nx, ny, nz) = sizes
    (bx, by, bz) = conductivity.shape
    count = nx * ny * nz
    mid = (nx * bx // 2 + 2, ny * by // 2, nz * bz // 2)
    low = (nx * bx // 4 + 2, ny * by // 4, nz * bz // 4)
    window = (3 * bx, 3 * by, bz + 128)
    kept = lambda shape: pltpu.VMEM(shape, jnp.float32)
    inner_mid = (mid[0] - 2, *mid[1:])
    sent = (bx * by // 32, 8, bz // 2)
    groups = (bx + 10 + 15) // 16
    scratch = [kept(window)] * 8 + [kept(mid)] * 8 + [kept(low)] * 8
    scratch += [kept(window), kept(inner_mid), kept(mid), kept((low[0] - 2, *low[1:]))]
    scratch += [kept(sent), kept(sent), kept((bx, by, bz))]
    scratch += [kept((count, *sent)), kept((count, *sent))]
    scratch += [kept((3, 2, groups, 3 * by, 128)), kept((3, 2, groups, 3 * by, 128))]
    dma = pltpu.SemaphoreType.DMA
    scratch += [dma((3, 9)), dma((3, 9)), dma((3, 2)), dma((3, 2)), dma((2, count)), dma((2, count))]
    shape = jax.ShapeDtypeStruct((bx, by, bz), jnp.float32)
    vmem = pl.BlockSpec(memory_space=pltpu.VMEM)
    return pl.pallas_call(
        functools.partial(kernel, sizes, (bx, by, bz)),
        out_shape=(shape, shape),
        in_specs=[vmem, vmem],
        out_specs=(vmem, vmem),
        scratch_shapes=scratch,
        compiler_params=pltpu.CompilerParams(
            collective_id=0, has_side_effects=True, vmem_limit_bytes=48 * 1024 * 1024
        ),
    )(conductivity, source)


def plan(conductivity, source):
    sizes = tuple(lax.axis_size(axis) for axis in ("gx", "gy", "gz"))
    (bx, by, bz) = conductivity.shape
    count = sizes[0] * sizes[1] * sizes[2]
    fits = bx == 8 and by == 8 and bz % 256 == 0 and sizes[1] % 2 == 0
    if fits and count > 1 and count * bx * by * bz // 8 * 4 * 16 <= 16 * 1024 * 1024:
        return gathered(sizes, conductivity, source)
    return body(conductivity, source)


def solution(mesh):
    in_specs = (P("gx", "gy", "gz"), P("gx", "gy", "gz"))
    out_specs = (P("gx", "gy", "gz"), P("gx", "gy", "gz"))
    return jax.shard_map(plan, mesh=mesh, in_specs=in_specs, out_specs=out_specs, check_vma=False)
```

profile of v0, /device:TPU:0, one launch (start us, length us, event | category | flops | bytes accessed | tf_op | source)
XLA Modules:
  0.0 64.1 jit_solution(13711965894932388073)
XLA Ops:
  0.6 0.0 copy-start
  0.6 0.8 %copy-done = f32[8,8,256]{2,1,0:T(8,128)S(1)} copy-done((f32[8,8,256]{2,1,0:T(8,128)S(1)}, f32[8,8,256]{2,1,0:T(8,128)}, u32[]{:S(2)}) %copy-start) | copy-done | bytes 65560
  1.5 0.0 copy-start.1
  1.5 0.8 %copy-done.1 = f32[8,8,256]{2,1,0:T(8,128)S(1)} copy-done((f32[8,8,256]{2,1,0:T(8,128)S(1)}, f32[8,8,256]{2,1,0:T(8,128)}, u32[]{:S(2)}) %copy-start.1) | copy-done | bytes 65560
  2.3 60.5 %shard_map.41 = (f32[8,8,256]{2,1,0:T(8,128)S(1)}, f32[8,8,256]{2,1,0:T(8,128)S(1)}) custom-call(f32[8,8,256]{2,1,0:T(8,128)S(1)} %copy-done, f32[8,8,256]{2,1,0:T(8,128)S(1)} %copy-done.1), custom_call_target="tpu_custom_call" | custom-call | tf_op jit(solution)/shard_map/pallas_call | solution.py:642
  62.8 0.6 copy.6
  63.5 0.6 copy.7
Async XLA Ops:
  0.6 0.8 %copy-start = (f32[8,8,256]{2,1,0:T(8,128)S(1)}, f32[8,8,256]{2,1,0:T(8,128)}, u32[]{:S(2)}) copy-start(f32[8,8,256]{2,1,0:T(8,128)} %refs_0_.1) | copy-start | bytes 196612
  1.5 0.8 %copy-start.1 = (f32[8,8,256]{2,1,0:T(8,128)S(1)}, f32[8,8,256]{2,1,0:T(8,128)}, u32[]{:S(2)}) copy-start(f32[8,8,256]{2,1,0:T(8,128)} %refs_1_.1) | copy-start | bytes 196612
where the time goes:
time: 64.3 us; the launch traced here: 64.1 us
  Pallas kernels  60.5 us (94%)
  local copies, waits for them, and re-layouts  2.93 us (5%)
  between operations  0.65 us (1%)
    pallas_call x1, Pallas kernels, gathered(): pl.pallas_call(functools.partial(kernel, sizes, (bx, by, bz)), out_shape=...  60.5 us
    unnamed x6, local copies, waits for them, and re-layouts  2.93 us

commit v1 on v0

--- a/solution.py
+++ b/solution.py
@@ -198,6 +198,44 @@
     return cycle(0, source)
 
 
+def part_of(values, size):
+    if size & (size - 1) == 0:
+        return values >> (size.bit_length() - 1)
+    return values // size
+
+
+def rest_of(values, size):
+    if size & (size - 1) == 0:
+        return values & (size - 1)
+    return values % size
+
+
+def fold(values, eighth):
+    side = jnp.where(eighth, values[8:16], values[16:24])
+    return jnp.concatenate([values[0:8], side], axis=0)
+
+
+def over(span, step):
+    if isinstance(span[0], int):
+        planes = span[1] - span[0]
+        if planes <= 4:
+            for p in range(*span):
+                step(p)
+            return
+        size = 2 if planes % 2 == 0 else 1
+        trips = planes // size
+    else:
+        size = 2
+        trips = (span[1] - span[0] + 1) >> 1
+
+    def body_of(i, carry):
+        for j in range(size):
+            step(span[0] + size * i + j)
+        return carry
+
+    lax.fori_loop(0, trips, body_of, 0)
+
+
 def cells(shape, dim):
     return lax.broadcasted_iota(jnp.int32, shape, dim)
 
@@ -242,58 +280,67 @@
 
 
 class Level:
-    def __init__(self, refs, scale, wraps):
+    def __init__(self, refs, scale, wide_refs=None):
         self.k, self.r, self.d, self.di, self.dg, self.e, self.f, self.g = refs
         self.scale = scale
         shape = self.k.shape[1:]
+        self.wide_refs = wide_refs
         self.edges = None
-        if not wraps:
+        if wide_refs is None:
             self.edges = [
                 (cells(shape, dim) == 0, cells(shape, dim) == shape[dim] - 1) for dim in (0, 1)
             ]
+        else:
+            self.eighth = cells((8, shape[1]), 0) < 4
+
+    def folded(self, values):
+        return values if self.wide_refs is None else fold(values, self.eighth)
 
     def diagonal(self, wide, near, inside):
-        def first(p, carry):
-            here, side = plane_sums(self.k[p], self.edges)
-            self.e[p] = here
-            self.g[p] = side
-            return carry
-
-        lax.fori_loop(wide[0], wide[1], first, 0)
-
-        def second(p, carry):
-            total = 128.0 * self.k[p] + self.e[p] + self.g[p - 1] + self.g[p + 1]
+        def first(p):
+            coeff = self.k[p] if self.wide_refs is None else self.wide_refs[0][p]
+            here, side = plane_sums(coeff, self.edges)
+            self.e[p] = self.folded(here)
+            self.g[p] = self.folded(side)
+            if self.wide_refs is not None:
+                self.k[p] = self.folded(coeff)
+
+        over(wide, first)
+
+        def second(p):
+            total = 128.0 * self.k[p] + self.e[p] + (self.g[p - 1] + self.g[p + 1])
             total = total * self.scale
             self.dg[p] = total
-            good = total > 0.0
+            good = (total > 0.0) & (self.k[p] > 0.0)
             if inside is not None:
                 good = good & inside
             self.di[p] = jnp.where(good, 1.0 / total, 0.0)
-            return carry
-
-        lax.fori_loop(near[0], near[1], second, 0)
+
+        over(near, second)
 
     def first_update(self, span, centre):
-        def step(p, carry):
+        def step(p):
             self.d[p] = self.r[p] * self.di[p] * (1.0 / centre)
-            return carry
-
-        lax.fori_loop(span[0], span[1], step, 0)
-
-    def apply(self, wide, near, pair):
-        def first(p, carry):
-            field = self.d[p]
-            coeff = self.k[p]
+
+        over(span, step)
+
+    def apply(self, wide, near, pair, whole=False):
+        def first(p):
+            field = self.wide_refs[1][p] if whole else self.d[p]
+            coeff = self.wide_refs[0][p] if whole else self.k[p]
             here, side = plane_sums(field, self.edges)
             here_k, side_k = plane_sums(coeff * field, self.edges)
-            self.e[p] = coeff * here + here_k
+            around = coeff * here + here_k
+            if whole:
+                around, side, side_k = (self.folded(part) for part in (around, side, side_k))
+                self.d[p] = self.folded(field)
+            self.e[p] = around
             self.f[p] = side
             self.g[p] = side_k
-            return carry
-
-        lax.fori_loop(wide[0], wide[1], first, 0)
-
-        def second(p, carry):
+
+        over(wide, first)
+
+        def second(p):
             field = self.d[p]
             around = self.e[p] + self.k[p] * (self.f[p - 1] + self.f[p + 1])
             around = around + (self.g[p - 1] + self.g[p + 1])
@@ -302,9 +349,8 @@
             if pair is not None:
                 fresh = pair[1] * (left * self.di[p])
                 self.d[p] = fresh if pair[0] == 0.0 else pair[0] * field + fresh
-            return carry
-
-        lax.fori_loop(near[0], near[1], second, 0)
+
+        over(near, second)
 
 
 def kernel(sizes, block, *refs):
@@ -315,10 +361,12 @@
     fine_refs = refs[4:12]
     mid_refs = refs[12:20]
     low_refs = refs[20:28]
-    (far, x_mid, b_mid, x_low) = refs[28:32]
-    (k_send, b_send, r_send, k_got, b_got) = refs[32:37]
-    (pack_out, pack_in) = refs[37:39]
-    (halo_out, halo_in, z_out, z_in, all_out, all_in) = refs[39:45]
+    (x_mid, b_mid, x_low) = refs[28:31]
+    (k_send, b_send, r_send, k_got, b_got) = refs[31:36]
+    (k_near, b_near, r_near, d_wide) = refs[36:40]
+    packs_out, packs_in = refs[40:43], refs[43:46]
+    (halo_out, halo_in, z_out, z_in, all_out, all_in) = refs[46:52]
+    (rows_keep, columns_keep) = refs[52:54]
     ix, iy, iz = lax.axis_index("gx"), lax.axis_index("gy"), lax.axis_index("gz")
     me = (ix * ny + iy) * nz + iz
     reach = 5
@@ -326,12 +374,18 @@
     def place(number):
         return (number // (ny * nz), (number // nz) % ny, number % nz)
 
-    for ref in (*fine_refs, *mid_refs, *low_refs, far):
-        def clear(p, carry, ref=ref):
+    def clear(ref, planes):
+        def step(p):
             ref[p] = jnp.zeros(ref.shape[1:], jnp.float32)
-            return carry
-
-        lax.fori_loop(0, ref.shape[0], clear, 0)
+
+        if isinstance(planes, list):
+            for p in planes:
+                step(p)
+        else:
+            over(planes, step)
+
+    for ref in (k_near, b_near, r_near):
+        clear(ref, (bx - reach - 1, 2 * bx + reach + 1))
 
     barrier = pltpu.get_barrier_semaphore()
 
@@ -344,14 +398,15 @@
     lax.fori_loop(1, count, greet, 0)
     pl.semaphore_wait(barrier, count - 1)
 
-    fine = Level(fine_refs, 0.5 / 30.0, True)
-    mid = Level(mid_refs, 0.5 / 4.0 / 30.0, False)
-    low = Level(low_refs, 0.5 / 16.0 / 30.0, False)
+    fine = Level(fine_refs, 0.5 / 30.0, (k_near, d_wide))
+    mid = Level(mid_refs, 0.5 / 4.0 / 30.0)
+    low = Level(low_refs, 0.5 / 16.0 / 30.0)
 
     def near_copy(source, target, which, dx, dy):
-        planes = bx if dx == 0 else reach
-        first_from = 0 if dx <= 0 else bx - reach
-        first_to = {0: bx, 1: bx - reach, -1: 2 * bx}[dx]
+        deep = reach if which == 0 else reach - 1
+        planes = bx if dx == 0 else deep
+        first_from = 0 if dx <= 0 else bx - deep
+        first_to = {0: bx, 1: bx - deep, -1: 2 * bx}[dx]
         row_to = {0: 0, 1: 2 * by, -1: by}[dy]
         number = (dx + 1) * 3 + dy + 1
         return pltpu.make_async_remote_copy(
@@ -384,14 +439,17 @@
             def _():
                 near_copy(source, target, which, dx, dy).wait_send()
 
-    lane = cells((3 * by, 128), 1)
-    z_planes = list(range(bx - reach, 2 * bx + reach))
-    groups = (len(z_planes) + 15) // 16
+    eighth = cells((8, bz), 0) < 4
+
+    def z_planes(which):
+        deep = reach if which == 0 else reach - 1
+        planes = list(range(bx - deep, 2 * bx + deep))
+        return [planes[i : i + 16] for i in range(0, len(planes), 16)]
 
     def z_copy(which, side):
         return pltpu.make_async_remote_copy(
-            src_ref=pack_out.at[which, side],
-            dst_ref=pack_in.at[which, side],
+            src_ref=packs_out[which].at[side],
+            dst_ref=packs_in[which].at[side],
             send_sem=z_out.at[which, side],
             recv_sem=z_in.at[which, side],
             device_id=(ix, iy, iz + (1 if side == 0 else -1)),
@@ -402,21 +460,25 @@
     from_there = (iz > 0, iz + 1 < nz)
 
     def z_start(window, which):
-        for group in range(groups):
-            up = jnp.zeros((3 * by, 128), jnp.float32)
-            down = jnp.zeros((3 * by, 128), jnp.float32)
-            for i, p in enumerate(z_planes[group * 16 : group * 16 + 16]):
-                mine = lane // 8 == i
+        pack = packs_out[which]
+        lane = cells(pack.shape[2:], 1)
+        for group, planes in enumerate(z_planes(which)):
+            up = jnp.zeros(pack.shape[2:], jnp.float32)
+            down = jnp.zeros(pack.shape[2:], jnp.float32)
+            for i, p in enumerate(planes):
+                mine = (lane >> 3) == i
                 up = jnp.where(mine, turn(window[p, :, bz - 128 : bz], 8 * i + 8, 1), up)
                 down = jnp.where(mine, turn(window[p, :, 0:128], 8 * i, 1), down)
-            pack_out[which, 0, group] = up
-            pack_out[which, 1, group] = down
+            pack[0, group] = up
+            pack[1, group] = down
         for side in (0, 1):
             @pl.when(to_there[side])
             def _():
                 z_copy(which, side).start()
 
     def z_finish(window, which):
+        pack = packs_in[which]
+        lane = cells(pack.shape[2:], 1)
         for side in (0, 1):
             @pl.when(from_there[side])
             def _():
@@ -424,19 +486,23 @@
 
             @pl.when(jnp.logical_not(from_there[side]))
             def _():
-                pack_in[which, side] = jnp.zeros(pack_in.shape[2:], jnp.float32)
+                pack[side] = jnp.zeros(pack.shape[1:], jnp.float32)
 
             @pl.when(to_there[side])
             def _():
                 z_copy(which, side).wait_send()
 
-        for group in range(groups):
-            below = pack_in[which, 0, group]
-            above = pack_in[which, 1, group]
-            for i, p in enumerate(z_planes[group * 16 : group * 16 + 16]):
+        for group, planes in enumerate(z_planes(which)):
+            below = pack[0, group]
+            above = pack[1, group]
+            for i, p in enumerate(planes):
                 window[p, :, bz : bz + 128] = jnp.where(
                     lane < 64, turn(above, -8 * i, 1), turn(below, -8 * i - 8, 1)
                 )
+
+    def fold_in(window):
+        for p in z_planes(1)[0]:
+            fine.r[p, :, 0:bz] = fold(window[p, :, 0:bz], eighth)
 
     def all_copy(source, target, which, peer, slot):
         return pltpu.make_async_remote_copy(
@@ -469,9 +535,10 @@
     half = bx // 2 * (by // 2)
     to_row, from_row = cells((half, bx * by), 0), cells((half, bx * by), 1)
     shrink = ones_where(
-        (from_row // by // 2 == to_row // (by // 2)) & (from_row % by // 2 == to_row % (by // 2))
+        (part_of(from_row, 2 * by) == part_of(to_row, by // 2))
+        & (rest_of(from_row, by) >> 1 == rest_of(to_row, by // 2))
     )
-    shrink_z = ones_where(cells((bz, bz // 2), 0) // 2 == cells((bz, bz // 2), 1))
+    shrink_z = ones_where(cells((bz, bz // 2), 0) >> 1 == cells((bz, bz // 2), 1))
 
     def coarse_block(values):
         flat = pick(pick(shrink, values.reshape(bx * by, bz)), shrink_z) * 0.125
@@ -491,17 +558,42 @@
                         target[(p, *at)] = jnp.where(row8 < 4, one, turn(two, 4, 0))
                         target[(p + 1, *at)] = jnp.where(row8 < 4, turn(one, 4, 0), two)
 
-    near_start(k_in, fine.k, 0)
-    near_start(b_in, fine.r, 1)
+    near_start(k_in, k_near, 0)
+    near_start(b_in, b_near, 1)
     k_send[...] = coarse_block(k_in[...])
+    k_near[bx : 2 * bx, 0:by, 0:bz] = k_in[...]
+    b_near[bx : 2 * bx, 0:by, 0:bz] = b_in[...]
+    edge = bx - reach - 1
+    for ref in fine_refs:
+        clear(ref, [edge, bx - 1, 2 * bx, 2 * bx + 1, 2 * bx + reach])
+        clear(ref, (edge, bx))
+        clear(ref, (2 * bx, 2 * bx + reach + 1))
+    clear(d_wide, [2 * bx + reach])
+    for ref in (mid.f, mid.g):
+        clear(ref, [0, ref.shape[0] - 1])
+    for ref in (low.f, low.g):
+        clear(ref, [0, ref.shape[0] - 1])
+    mx, my, mz = mid.k.shape[0] - 2, mid.k.shape[1], mid.k.shape[2]
+    wide = bx + bx // 2
+    mid_x = ix * (bx // 2) - bx // 2
+    for q in range(wide):
+        shape = (3 * by, mx * my)
+        fine_row, mid_row = cells(shape, 0), cells(shape, 1)
+        fine_y = iy * by + jnp.where(fine_row < 2 * by, fine_row, fine_row - 3 * by)
+        target = (mid_x + q) * my + (fine_y >> 1)
+        good = (fine_y >= 0) & (fine_y < ny * by) & (mid_x + q >= 0) & (mid_x + q < mx)
+        rows_keep[q] = jnp.where((mid_row == target) & good, 1.0, 0.0)
+    shape = (mz, bz + 128)
+    fine_col = cells(shape, 1)
+    fine_z = iz * bz + jnp.where(fine_col < bz + 64, fine_col, fine_col - (bz + 128))
+    columns_keep[...] = ones_where((fine_z >> 1) == cells(shape, 0))
+    near_wait(k_in, k_near, 0)
+    z_start(k_near, 0)
+    near_wait(b_in, b_near, 1)
+    fold_in(b_near)
+    z_start(fine.r, 1)
     all_start(k_send, k_got, 0)
-    fine.k[bx : 2 * bx, 0:by, 0:bz] = k_in[...]
-    fine.r[bx : 2 * bx, 0:by, 0:bz] = b_in[...]
-    near_wait(k_in, fine.k, 0)
-    z_start(fine.k, 0)
-    near_wait(b_in, fine.r, 1)
-    z_start(fine.r, 1)
-    z_finish(fine.k, 0)
+    z_finish(k_near, 0)
 
     def span(width):
         return (
@@ -509,10 +601,10 @@
             jnp.minimum(2 * bx + width, bx + (nx - ix) * bx),
         )
 
-    plane = (3 * by, bz + 128)
+    plane = (2 * by, bz + 128)
     row, col = cells(plane, 0), cells(plane, 1)
     inside = (
-        (row < by) | ((row < 2 * by) & (iy + 1 < ny)) | ((row >= 2 * by) & (iy > 0))
+        (row < by) | ((row < by + 4) & (iy + 1 < ny)) | ((row >= by + 4) & (iy > 0))
     ) & ((col < bz) | ((col < bz + 64) & (iz + 1 < nz)) | ((col >= bz + 64) & (iz > 0)))
     fine.diagonal(span(5), span(4), inside)
     z_finish(fine.r, 1)
@@ -530,18 +622,19 @@
     r_send[...] = fine.r[own]
     b_send[...] = coarse_block(r_send[...])
     all_start(b_send, b_got, 1)
-    near_start(r_send, far, 2)
-    far[own] = r_send[...]
-
-    mx, my, mz = mid.k.shape[0] - 2, mid.k.shape[1], mid.k.shape[2]
+    near_start(r_send, r_near, 2)
+    r_near[own] = r_send[...]
+
     cx, cy, cz = mx // 2, my // 2, mz // 2
     mid_span, low_span = (1, mx + 1), (1, cx + 1)
     all_wait(k_send, k_got, 0)
     unpack(k_got, mid.k)
     mid.diagonal(mid_span, mid_span, None)
     big, small = cells((cx * cy, mx * my), 1), cells((cx * cy, mx * my), 0)
-    join = ones_where((big // my // 2 == small // cy) & (big % my // 2 == small % cy))
-    join_z = ones_where(cells((mz, cz), 0) // 2 == cells((mz, cz), 1))
+    join = ones_where(
+        (part_of(big, 2 * my) == part_of(small, cy)) & (rest_of(big, my) >> 1 == rest_of(small, cy))
+    )
+    join_z = ones_where(cells((mz, cz), 0) >> 1 == cells((mz, cz), 1))
 
     def to_low(values):
         flat = pick(join, pick(values.reshape(mx * my, mz), join_z)) * 0.125
@@ -561,8 +654,9 @@
         if pair is not None:
             x_mid[...] += mid.d[1 : mx + 1]
 
-    near_wait(r_send, far, 2)
-    z_start(far, 2)
+    near_wait(r_send, r_near, 2)
+    fold_in(r_near)
+    z_start(fine.r, 2)
 
     low.r[1 : cx + 1] = to_low(mid.r[1 : mx + 1])
     low_centre, low_weights = chebyshev_coefs(COARSE_DEGREE, coarse_low)
@@ -572,11 +666,11 @@
         low.apply(low_span, low_span, pair)
         x_low[...] += low.d[1 : cx + 1]
 
+    big, small = cells((mx * my, cx * cy), 0), cells((mx * my, cx * cy), 1)
     spread = ones_where(
-        (cells((mx * my, cx * cy), 0) // my // 2 == cells((mx * my, cx * cy), 1) // cy)
-        & (cells((mx * my, cx * cy), 0) % my // 2 == cells((mx * my, cx * cy), 1) % cy)
+        (part_of(big, 2 * my) == part_of(small, cy)) & (rest_of(big, my) >> 1 == rest_of(small, cy))
     )
-    spread_z = ones_where(cells((cz, mz), 0) == cells((cz, mz), 1) // 2)
+    spread_z = ones_where(cells((cz, mz), 0) == cells((cz, mz), 1) >> 1)
     fixed = pick(spread, pick(x_low[...].reshape(cx * cy, cz), spread_z))
     mid.d[1 : mx + 1] = x_mid[...] + fixed.reshape(mx, my, mz)
     mid.r[1 : mx + 1] = b_mid[1 : mx + 1]
@@ -587,29 +681,14 @@
         mid.apply(mid_span, mid_span, pair)
         x_mid[...] += mid.d[1 : mx + 1]
 
-    z_finish(far, 2)
-    wide = bx + bx // 2
-    shape = (wide * 3 * by, mx * my)
-    fine_row, mid_row = cells(shape, 0) % (3 * by), cells(shape, 1)
-    fine_y = iy * by + jnp.where(fine_row < 2 * by, fine_row, fine_row - 3 * by)
-    mid_x = ix * (bx // 2) + cells(shape, 0) // (3 * by) - bx // 2
-    rows = ones_where((mid_row // my == mid_x) & (2 * (mid_row % my) == fine_y - fine_y % 2))
-    shape = (mz, bz + 128)
-    fine_col = cells(shape, 1)
-    fine_z = iz * bz + jnp.where(fine_col < bz + 64, fine_col, fine_col - (bz + 128))
-    columns = ones_where((fine_z >= 2 * cells(shape, 0)) & (fine_z <= 2 * cells(shape, 0) + 1))
-    fixed = pick(rows, pick(x_mid[...].reshape(mx * my, mz), columns))
+    z_finish(fine.r, 2)
+    rows = rows_keep[...].reshape(wide * 3 * by, mx * my).astype(jnp.bfloat16)
+    fixed = pick(rows, pick(x_mid[...].reshape(mx * my, mz), columns_keep[...]))
     fixed = fixed.reshape(wide, 3 * by, bz + 128)
     for p in range(bx - reach, 2 * bx + reach):
-        fine.d[p] = fixed[p // 2]
-    x_out[...] += fine.d[own]
-
-    def restore(p, carry):
-        fine.r[p] = far[p]
-        return carry
-
-    lax.fori_loop(*span(4), restore, 0)
-    fine.apply(span(5), span(4), (0.0, 1.0 / centre))
+        d_wide[p] = fixed[p // 2]
+    x_out[...] += d_wide[own]
+    fine.apply(span(5), span(4), (0.0, 1.0 / centre), True)
     x_out[...] += fine.d[own]
     for number in range(DEGREE):
         pair = weights[number] if number < DEGREE - 1 else None
@@ -626,17 +705,21 @@
     mid = (nx * bx // 2 + 2, ny * by // 2, nz * bz // 2)
     low = (nx * bx // 4 + 2, ny * by // 4, nz * bz // 4)
     window = (3 * bx, 3 * by, bz + 128)
+    narrow = (3 * bx, 2 * by, bz + 128)
     kept = lambda shape: pltpu.VMEM(shape, jnp.float32)
     inner_mid = (mid[0] - 2, *mid[1:])
     sent = (bx * by // 32, 8, bz // 2)
-    groups = (bx + 10 + 15) // 16
-    scratch = [kept(window)] * 8 + [kept(mid)] * 8 + [kept(low)] * 8
-    scratch += [kept(window), kept(inner_mid), kept(mid), kept((low[0] - 2, *low[1:]))]
+    scratch = [kept(narrow)] * 8 + [kept(mid)] * 8 + [kept(low)] * 8
+    scratch += [kept(inner_mid), kept(mid), kept((low[0] - 2, *low[1:]))]
     scratch += [kept(sent), kept(sent), kept((bx, by, bz))]
     scratch += [kept((count, *sent)), kept((count, *sent))]
-    scratch += [kept((3, 2, groups, 3 * by, 128)), kept((3, 2, groups, 3 * by, 128))]
+    scratch += [kept(window)] * 4
+    packs = [kept((2, 2, 3 * by, 128)), kept((2, 1, 2 * by, 128)), kept((2, 1, 2 * by, 128))]
+    scratch += packs + packs
     dma = pltpu.SemaphoreType.DMA
     scratch += [dma((3, 9)), dma((3, 9)), dma((3, 2)), dma((3, 2)), dma((2, count)), dma((2, count))]
+    scratch += [kept((bx + bx // 2, 3 * by, inner_mid[0] * inner_mid[1]))]
+    scratch += [pltpu.VMEM((inner_mid[2], bz + 128), jnp.bfloat16)]
     shape = jax.ShapeDtypeStruct((bx, by, bz), jnp.float32)
     vmem = pl.BlockSpec(memory_space=pltpu.VMEM)
     return pl.pallas_call(

time: 64.3 us -> 49.8 us (0.77)
  Pallas kernels: 60.5 us -> 46 us
    pallas_call x1, Pallas kernels: 60.5 us -> 46 us  [gathered(): pl.pallas_call(functools.partial(kernel, sizes, (bx, by, bz)), out_shape=...]
where the time goes in v1:
time: 49.8 us; the launch traced here: 49.6 us
  Pallas kernels  46 us (92%)
  local copies, waits for them, and re-layouts  2.93 us (6%)
  between operations  0.65 us (1%)
    pallas_call x1, Pallas kernels, gathered(): pl.pallas_call(functools.partial(kernel, sizes, (bx, by, bz)), out_shape=...  46 us
    unnamed x6, local copies, waits for them, and re-layouts  2.93 us

profile of v1, /device:TPU:0, one launch (start us, length us, event | category | flops | bytes accessed | tf_op | source)
XLA Modules:
  0.0 49.6 jit_solution(2353074703695070432)
XLA Ops:
  0.6 0.0 copy-start
  0.6 0.8 %copy-done = f32[8,8,256]{2,1,0:T(8,128)S(1)} copy-done((f32[8,8,256]{2,1,0:T(8,128)S(1)}, f32[8,8,256]{2,1,0:T(8,128)}, u32[]{:S(2)}) %copy-start) | copy-done | bytes 65560
  1.5 0.0 copy-start.1
  1.5 0.8 %copy-done.1 = f32[8,8,256]{2,1,0:T(8,128)S(1)} copy-done((f32[8,8,256]{2,1,0:T(8,128)S(1)}, f32[8,8,256]{2,1,0:T(8,128)}, u32[]{:S(2)}) %copy-start.1) | copy-done | bytes 65560
  2.3 46.0 %shard_map.41 = (f32[8,8,256]{2,1,0:T(8,128)S(1)}, f32[8,8,256]{2,1,0:T(8,128)S(1)}) custom-call(f32[8,8,256]{2,1,0:T(8,128)S(1)} %copy-done, f32[8,8,256]{2,1,0:T(8,128)S(1)} %copy-done.1), custom_call_target="tpu_custom_call" | custom-call | tf_op jit(solution)/shard_map/pallas_call | solution.py:725
  48.4 0.6 %copy.6 = f32[8,8,256]{2,1,0:T(8,128)} copy(f32[8,8,256]{2,1,0:T(8,128)S(1)} %get-tuple-element.4) | data formatting | bytes 131072
  49.0 0.6 %copy.7 = f32[8,8,256]{2,1,0:T(8,128)} copy(f32[8,8,256]{2,1,0:T(8,128)S(1)} %get-tuple-element.5) | data formatting | bytes 131072
Async XLA Ops:
  0.6 0.8 %copy-start = (f32[8,8,256]{2,1,0:T(8,128)S(1)}, f32[8,8,256]{2,1,0:T(8,128)}, u32[]{:S(2)}) copy-start(f32[8,8,256]{2,1,0:T(8,128)} %refs_0_.1) | copy-start | bytes 196612
  1.5 0.8 %copy-start.1 = (f32[8,8,256]{2,1,0:T(8,128)S(1)}, f32[8,8,256]{2,1,0:T(8,128)}, u32[]{:S(2)}) copy-start(f32[8,8,256]{2,1,0:T(8,128)} %refs_1_.1) | copy-start | bytes 196612

commit v2 on v1

--- a/solution.py
+++ b/solution.py
@@ -222,7 +222,7 @@
             for p in range(*span):
                 step(p)
             return
-        size = 2 if planes % 2 == 0 else 1
+        size = 4 if planes % 4 == 0 else 2 if planes % 2 == 0 else 1
         trips = planes // size
     else:
         size = 2

time: 49.8 us -> 48.4 us (0.972)
  Pallas kernels: 46 us -> 44.6 us
    pallas_call x1, Pallas kernels: 46 us -> 44.6 us  [gathered(): pl.pallas_call(functools.partial(kernel, sizes, (bx, by, bz)), out_shape=...]
where the time goes in v2:
time: 48.4 us; the launch traced here: 48.2 us
  Pallas kernels  44.6 us (92%)
  local copies, waits for them, and re-layouts  2.93 us (6%)
  between operations  0.65 us (1%)
    pallas_call x1, Pallas kernels, gathered(): pl.pallas_call(functools.partial(kernel, sizes, (bx, by, bz)), out_shape=...  44.6 us
    unnamed x6, local copies, waits for them, and re-layouts  2.93 us

profile of v2, /device:TPU:0, one launch (start us, length us, event | category | flops | bytes accessed | tf_op | source)
XLA Modules:
  0.0 48.2 jit_solution(4048656580513549598)
XLA Ops:
  0.6 0.0 copy-start
  0.6 0.8 %copy-done = f32[8,8,256]{2,1,0:T(8,128)S(1)} copy-done((f32[8,8,256]{2,1,0:T(8,128)S(1)}, f32[8,8,256]{2,1,0:T(8,128)}, u32[]{:S(2)}) %copy-start) | copy-done | bytes 65560
  1.5 0.0 copy-start.1
  1.5 0.8 %copy-done.1 = f32[8,8,256]{2,1,0:T(8,128)S(1)} copy-done((f32[8,8,256]{2,1,0:T(8,128)S(1)}, f32[8,8,256]{2,1,0:T(8,128)}, u32[]{:S(2)}) %copy-start.1) | copy-done | bytes 65560
  2.3 44.6 %shard_map.41 = (f32[8,8,256]{2,1,0:T(8,128)S(1)}, f32[8,8,256]{2,1,0:T(8,128)S(1)}) custom-call(f32[8,8,256]{2,1,0:T(8,128)S(1)} %copy-done, f32[8,8,256]{2,1,0:T(8,128)S(1)} %copy-done.1), custom_call_target="tpu_custom_call" | custom-call | tf_op jit(solution)/shard_map/pallas_call | solution.py:725
  46.9 0.6 %copy.6 = f32[8,8,256]{2,1,0:T(8,128)} copy(f32[8,8,256]{2,1,0:T(8,128)S(1)} %get-tuple-element.4) | data formatting | bytes 131072
  47.6 0.6 %copy.7 = f32[8,8,256]{2,1,0:T(8,128)} copy(f32[8,8,256]{2,1,0:T(8,128)S(1)} %get-tuple-element.5) | data formatting | bytes 131072
Async XLA Ops:
  0.6 0.8 %copy-start = (f32[8,8,256]{2,1,0:T(8,128)S(1)}, f32[8,8,256]{2,1,0:T(8,128)}, u32[]{:S(2)}) copy-start(f32[8,8,256]{2,1,0:T(8,128)} %refs_0_.1) | copy-start | bytes 196612
  1.5 0.8 %copy-start.1 = (f32[8,8,256]{2,1,0:T(8,128)S(1)}, f32[8,8,256]{2,1,0:T(8,128)}, u32[]{:S(2)}) copy-start(f32[8,8,256]{2,1,0:T(8,128)} %refs_1_.1) | copy-start | bytes 196612
